TPU v7x, 32 devices: a whole 2x2x4 slice. The times are simulated.
32 devices in a mesh: rows: 16 (over z, x, core), inner: 2 (over y).
Axes of the slice: x: 2, y: 2, z: 4, core: 2. Of those that a mesh axis runs over, the one named last changes fastest.
Arguments:
- blocks: bfloat16 [16, 16, 256, 256], P('rows'), may hold values from -0.375 to 0.375
- columns: int32 [16, 16], replicated, may hold values from -1 to 15, as said below
Outputs:
- purified: float32 [16, 16, 256, 256], P('rows', None, 'inner')
Inputs may be any that keep to these rules, and one draw needn't show every extreme that they name: Each entry of row i that is not -1 is (i + d) mod 16 for an offset d with -16 <= 2 * d < 16; the entries of a row are distinct and stand before its -1 entries; every row lists its diagonal block; some row lists 16 columns.
All inputs are finite; a program needn't handle non-finite values.
Results may differ from a plain program's by a relative error of at most 0.0055.
Values may be sent and summed in bfloat16 or wider, within the bound.
A program may use at most 128 MiB of HBM per device.

v0:
```python
import jax
import jax.numpy as jnp
from jax import lax
from jax.sharding import PartitionSpec as P


def from_behind(value, axis, steps):
    count = lax.axis_size(axis)
    pairs = [(source, (source + steps) % count) for source in range(count)]
    return lax.ppermute(value, axis, pairs)


def live_table(columns):
    nrows, band_width = columns.shape
    half_band = band_width // 2
    row_ids = jnp.arange(nrows, dtype=jnp.int32)
    target = (
        row_ids[:, None] + jnp.arange(band_width, dtype=jnp.int32)[None, :] - half_band
    ) % nrows
    return jnp.any(columns[:, None, :] == target[:, :, None], axis=2)


def slot_shift(piece, delta):
    band_width = piece.shape[1]
    if delta >= 0:
        return jnp.concatenate([piece[:, delta:], jnp.zeros_like(piece[:, :delta])], axis=1)
    return jnp.concatenate(
        [jnp.zeros_like(piece[:, :-delta]), piece[:, : band_width + delta]], axis=1
    )


def fetch_band(row_slab, below, above, block_rows, second):
    band_width = row_slab.shape[1]
    pieces = []
    for offset in range(-below, above + 1):
        if offset == 0:
            pieces.append(row_slab)
            continue
        trimmed = (abs(offset) - 1) * block_rows + 1
        if offset > 0:
            outgoing = row_slab[:, : band_width - trimmed]
        else:
            outgoing = row_slab[:, trimmed:]
        if second:
            incoming = from_behind(outgoing, "rows", -offset)
        else:
            incoming = from_behind(outgoing, "rows", -offset)
        filler = jnp.zeros_like(row_slab[:, :trimmed])
        if offset > 0:
            pieces.append(jnp.concatenate([incoming, filler], axis=1))
        else:
            pieces.append(jnp.concatenate([filler, incoming], axis=1))
    return jnp.concatenate(pieces, axis=0)


def merge_groups(totals):
    rounded = lax.optimization_barrier(totals.astype(jnp.bfloat16))
    return jnp.sum(rounded.astype(jnp.float32), axis=0)


def dense_terms(left, window, window_base, groups):
    block_rows, band_width, block_size, inner_width = left.shape
    out_width = window.shape[3]
    half_band = band_width // 2
    group_width = inner_width // groups
    stacked = jnp.stack(
        [
            slot_shift(
                window[window_base + offset : window_base + offset + block_rows], half_band - offset
            )
            for offset in range(band_width)
        ],
        axis=1,
    )
    left_groups = left.reshape(block_rows, band_width, block_size, groups, group_width)
    right_groups = stacked.reshape(
        block_rows, band_width, band_width, groups, group_width, out_width
    )
    totals = jnp.einsum(
        "ramcq,rascqn->crsmn", left_groups, right_groups, preferred_element_type=jnp.float32
    )
    return merge_groups(totals)


def band_terms(left, window, window_base, groups):
    return dense_terms(left, window, window_base, groups)


def per_device(blocks, columns):
    block_rows, band_width, block_size, _ = blocks.shape
    half_band = band_width // 2
    inner_count = lax.axis_size("inner")
    slab_width = block_size // inner_count
    inner_index = lax.axis_index("inner")
    row_owner = lax.axis_index("rows")
    live_own = lax.dynamic_slice_in_dim(live_table(columns), row_owner * block_rows, block_rows, 0)
    live_slots = live_own[:, :, None, None]
    masked = jnp.where(live_slots, blocks, jnp.zeros_like(blocks))
    below = -(-half_band // block_rows)
    above = -(-(half_band - 1) // block_rows)
    window_base = below * block_rows - half_band
    row_slab = lax.dynamic_slice_in_dim(masked, inner_index * slab_width, slab_width, 3)
    window = fetch_band(row_slab, below, above, block_rows, False)
    square = band_terms(masked, window, window_base, inner_count)
    square = jnp.where(live_slots, square, jnp.float32(0.0)).astype(jnp.bfloat16)
    second_window = fetch_band(square, below, above, block_rows, True)
    cubed = band_terms(masked, second_window, window_base, inner_count)
    cubed = jnp.where(live_slots, cubed, jnp.float32(0.0))
    column_slabs = 3.0 * square.astype(jnp.float32) - 2.0 * cubed
    return lax.all_to_all(
        column_slabs.astype(jnp.bfloat16), "inner", split_axis=2, concat_axis=3, tiled=True
    ).astype(column_slabs.dtype)


def solution(mesh):
    in_specs = (P("rows", None, None, None), P())
    out_specs = P("rows", None, "inner", None)
    return jax.shard_map(
        per_device, mesh=mesh, in_specs=in_specs, out_specs=out_specs, check_vma=False
    )
```

profile of v0, /device:TPU:10, one launch (start us, length us, event | category | flops | bytes accessed | tf_op | source)
XLA Modules:
  0.0 719.0 jit_solution(8122213784533948527)
XLA Ops:
  16.7 87.0 %collective-permute-done = bf16[1,8,256,128]{3,2,1,0:T(8,128)(2,1)} collective-permute-done((bf16[1,8,256,128]{3,2,1,0:T(8,128)(2,1)}, bf16[1,8,256,128]{3,2,1,0:T(8,128)(2,1)}, u32[]{:S(2)}, u32[]{:S(2)}) %collective-permute-start) | collective-permute-done | bytes 524320 | tf_op jit(solution)/shard_map/ppermute | solution.py:10
  104.6 5.9 collective-permute-start.5
  111.9 18.5 %collective-permute-done.14 = bf16[1,9,256,128]{3,2,1,0:T(8,128)(2,1)S(1)} collective-permute-done((bf16[1,9,256,128]{3,2,1,0:T(8,128)(2,1)}, bf16[1,9,256,128]{3,2,1,0:T(8,128)(2,1)S(1)}, u32[]{:S(2)}, u32[]{:S(2)}) %collective-permute-start.14) | collective-permute-done | bytes 589856 | tf_op jit(solution)/shard_map/ppermute | solution.py:10
  130.5 19.3 %collective-permute-start.4 = (bf16[1,12,256,128]{3,2,1,0:T(8,128)(2,1)}, bf16[1,12,256,128]{3,2,1,0:T(8,128)(2,1)}, u32[]{:S(2)}, u32[]{:S(2)}) collective-permute-start(bf16[1,12,256,128]{3,2,1,0:T(8,128)(2,1)} %get-tuple-element.12), channel_id=1, source_target_pairs={{0,8},{2,10},{4,12},{6,14},{8,16},{10,18},{12,20},{14,22},{16,24},... | collective-permute-start | bytes 2359304 | tf_op jit(solution)/shard_map/ppermute | solution.py:10
  151.9 4.0 collective-permute-start.10
  157.6 53.3 %collective-permute-done.12 = bf16[1,11,256,128]{3,2,1,0:T(8,128)(2,1)} collective-permute-done((bf16[1,11,256,128]{3,2,1,0:T(8,128)(2,1)}, bf16[1,11,256,128]{3,2,1,0:T(8,128)(2,1)}, u32[]{:S(2)}, u32[]{:S(2)}) %collective-permute-start.12) | collective-permute-done | bytes 720928 | tf_op jit(solution)/shard_map/ppermute | solution.py:10
  210.9 11.4 %collective-permute-done.4 = bf16[1,12,256,128]{3,2,1,0:T(8,128)(2,1)} collective-permute-done((bf16[1,12,256,128]{3,2,1,0:T(8,128)(2,1)}, bf16[1,12,256,128]{3,2,1,0:T(8,128)(2,1)}, u32[]{:S(2)}, u32[]{:S(2)}) %collective-permute-start.4) | collective-permute-done | bytes 786464 | tf_op jit(solution)/shard_map/ppermute | solution.py:10
  225.0 3.1 collective-permute-start.9
  261.0 2.6 constant_dynamic-update-slice_fusion.11
  272.7 2.5 constant_dynamic-update-slice_fusion.10
  302.3 2.5 constant_dynamic-update-slice_fusion.5
  307.3 2.5 constant_dynamic-update-slice_fusion.3
  309.8 2.6 constant_dynamic-update-slice_fusion.2
  314.8 10.9 %fusion.14 = bf16[2,1,16,256,128]{3,4,2,0,1:T(8,128)(2,1)S(1)} fusion(bf16[16,256,2,128,1]{3,2,1,0,4:T(2,128)(2,1)} %bitcast.123, bf16[1,16,16,2,128,128]{4,5,1,2,3,0:T(8,128)(2,1)} %constant_dynamic-update-slice_fusion), kind=kOutput, calls=%fused_computation.19 | convolution fusion | flops 4296015872 | bytes 20971520 | tf_op jit(solution)/shard_map/ramcq,rascqn->crsmn/dot_general | solution.py:79
  331.3 2.6 collective-permute-start.17
  334.5 94.1 %collective-permute-done.15 = bf16[1,8,256,128]{2,3,1,0:T(8,128)(2,1)S(1)} collective-permute-done((bf16[1,8,256,128]{2,3,1,0:T(8,128)(2,1)S(1)}, bf16[1,8,256,128]{2,3,1,0:T(8,128)(2,1)S(1)}, u32[]{:S(2)}, u32[]{:S(2)}) %collective-permute-start.15) | collective-permute-done | bytes 524320 | tf_op jit(solution)/shard_map/ppermute | solution.py:10
  430.5 13.2 %collective-permute-start.27 = (bf16[1,11,256,128]{2,3,1,0:T(8,128)(2,1)S(1)}, bf16[1,11,256,128]{2,3,1,0:T(8,128)(2,1)S(1)}, u32[]{:S(2)}, u32[]{:S(2)}) collective-permute-start(bf16[1,11,256,128]{2,3,1,0:T(8,128)(2,1)S(1)} %get-tuple-element.23), channel_id=1, source_target_pairs={{0,22},{2,24},{4,26},{6,28},{8,30},{10,0},{12,2},{14,4},{16,6},{18... | collective-permute-start | bytes 2162696 | tf_op jit(solution)/shard_map/ppermute | solution.py:10
  444.7 6.8 collective-permute-done.17
  453.2 28.1 %collective-permute-done.18 = bf16[1,11,256,128]{2,3,1,0:T(8,128)(2,1)S(1)} collective-permute-done((bf16[1,11,256,128]{2,3,1,0:T(8,128)(2,1)S(1)}, bf16[1,11,256,128]{2,3,1,0:T(8,128)(2,1)S(1)}, u32[]{:S(2)}, u32[]{:S(2)}) %collective-permute-start.18) | collective-permute-done | bytes 720928 | tf_op jit(solution)/shard_map/ppermute | solution.py:10
  481.3 3.1 collective-permute-start.21
  484.5 56.1 %collective-permute-done.27 = bf16[1,11,256,128]{2,3,1,0:T(8,128)(2,1)S(1)} collective-permute-done((bf16[1,11,256,128]{2,3,1,0:T(8,128)(2,1)S(1)}, bf16[1,11,256,128]{2,3,1,0:T(8,128)(2,1)S(1)}, u32[]{:S(2)}, u32[]{:S(2)}) %collective-permute-start.27) | collective-permute-done | bytes 720928 | tf_op jit(solution)/shard_map/ppermute | solution.py:10
  542.2 25.9 %collective-permute-start.22 = (bf16[1,15,256,128]{2,3,1,0:T(8,128)(2,1)}, bf16[1,15,256,128]{2,3,1,0:T(8,128)(2,1)}, u32[]{:S(2)}, u32[]{:S(2)}) collective-permute-start(bf16[1,15,256,128]{2,3,1,0:T(8,128)(2,1)} %get-tuple-element.32), channel_id=1, source_target_pairs={{0,2},{2,4},{4,6},{6,8},{8,10},{10,12},{12,14},{14,16},{16,18},{18... | collective-permute-start | bytes 2949128 | tf_op jit(solution)/shard_map/ppermute | solution.py:10
  587.0 2.5 constant_dynamic-update-slice_fusion.29
  661.9 2.6 copy.171
  664.5 2.6 constant_dynamic-update-slice_fusion.23
  671.0 2.5 constant_dynamic-update-slice_fusion.21
  676.0 2.5 constant_dynamic-update-slice_fusion.19
  678.5 2.6 constant_dynamic-update-slice_fusion.18
  681.1 2.5 constant_dynamic-update-slice_fusion.17
  684.8 8.4 %fusion.19 = bf16[2,1,16,256,128]{3,4,2,0,1:T(8,128)(2,1)S(1)} fusion(bf16[16,256,2,128,1]{3,2,1,0,4:T(2,128)(2,1)S(1)} %bitcast.124, bf16[1,16,16,2,128,128]{4,5,1,2,3,0:T(8,128)(2,1)} %constant_dynamic-update-slice_fusion.16), kind=kOutput, calls=%fused_computation.20 | convolution fusion | flops 4296015872 | bytes 20971520 | tf_op jit(solution)/shard_map/ramcq,rascqn->crsmn/dot_general | solution.py:79
  695.2 18.1 %all_to_all.4 = bf16[1,16,256,128]{3,1,0,2:T(8,128)(2,1)S(1)} all-to-all(bf16[1,16,256,128]{3,1,0,2:T(8,128)(2,1)S(1)} %copy.179), channel_id=1, replica_groups=mesh['rows'=16,'inner'=2] {'inner'}, dimensions={2} | all-to-all | bytes 2097152 | tf_op jit(solution)/shard_map/all_to_all | solution.py:110
  715.7 2.9 copy.182
  (202 shorter events, 214.5 us)
Async XLA Ops:
  4.2 99.5 %collective-permute-start.1 = (bf16[1,9,256,128]{3,2,1,0:T(8,128)(2,1)}, bf16[1,9,256,128]{3,2,1,0:T(8,128)(2,1)S(1)}, u32[]{:S(2)}, u32[]{:S(2)}) collective-permute-start(bf16[1,9,256,128]{3,2,1,0:T(8,128)(2,1)} %get-tuple-element.6), channel_id=1, source_target_pairs={{0,14},{2,16},{4,18},{6,20},{8,22},{10,24},{12,26},{14,28},{16,30}... | collective-permute-start | bytes 1769480 | tf_op jit(solution)/shard_map/ppermute | solution.py:10
  7.1 96.6 %collective-permute-start = (bf16[1,8,256,128]{3,2,1,0:T(8,128)(2,1)}, bf16[1,8,256,128]{3,2,1,0:T(8,128)(2,1)}, u32[]{:S(2)}, u32[]{:S(2)}) collective-permute-start(bf16[1,8,256,128]{3,2,1,0:T(8,128)(2,1)} %constant_dynamic-slice_fusion.14), channel_id=1, source_target_pairs={{0,16},{2,18},{4,20},{6,22},{8,24},{10,26},{12,28},{14,30},{16,0},... | collective-permute-start | bytes 1572872 | tf_op jit(solution)/shard_map/ppermute | solution.py:10
  9.1 140.7 %collective-permute-start.2 = (bf16[1,10,256,128]{3,2,1,0:T(8,128)(2,1)}, bf16[1,10,256,128]{3,2,1,0:T(8,128)(2,1)}, u32[]{:S(2)}, u32[]{:S(2)}) collective-permute-start(bf16[1,10,256,128]{3,2,1,0:T(8,128)(2,1)} %get-tuple-element.8), channel_id=1, source_target_pairs={{0,12},{2,14},{4,16},{6,18},{8,20},{10,22},{12,24},{14,26},{16,28}... | collective-permute-start | bytes 1966088 | tf_op jit(solution)/shard_map/ppermute | solution.py:10
  11.3 138.9 %collective-permute-start.13 = (bf16[1,10,256,128]{3,2,1,0:T(8,128)(2,1)}, bf16[1,10,256,128]{3,2,1,0:T(8,128)(2,1)}, u32[]{:S(2)}, u32[]{:S(2)}) collective-permute-start(bf16[1,10,256,128]{3,2,1,0:T(8,128)(2,1)} %get-tuple-element.7), channel_id=1, source_target_pairs={{0,20},{2,22},{4,24},{6,26},{8,28},{10,30},{12,0},{14,2},{16,4},{1... | collective-permute-start | bytes 1966088 | tf_op jit(solution)/shard_map/ppermute | solution.py:10
  12.0 118.4 %collective-permute-start.14 = (bf16[1,9,256,128]{3,2,1,0:T(8,128)(2,1)}, bf16[1,9,256,128]{3,2,1,0:T(8,128)(2,1)S(1)}, u32[]{:S(2)}, u32[]{:S(2)}) collective-permute-start(bf16[1,9,256,128]{3,2,1,0:T(8,128)(2,1)} %get-tuple-element.5), channel_id=1, source_target_pairs={{0,18},{2,20},{4,22},{6,24},{8,26},{10,28},{12,30},{14,0},{16,2},{... | collective-permute-start | bytes 1769480 | tf_op jit(solution)/shard_map/ppermute | solution.py:10
  103.7 48.2 %collective-permute-start.3 = (bf16[1,11,256,128]{3,2,1,0:T(8,128)(2,1)}, bf16[1,11,256,128]{3,2,1,0:T(8,128)(2,1)}, u32[]{:S(2)}, u32[]{:S(2)}) collective-permute-start(bf16[1,11,256,128]{3,2,1,0:T(8,128)(2,1)} %get-tuple-element.10), channel_id=1, source_target_pairs={{0,10},{2,12},{4,14},{6,16},{8,18},{10,20},{12,22},{14,24},{16,26}... | collective-permute-start | bytes 2162696 | tf_op jit(solution)/shard_map/ppermute | solution.py:10
  104.6 119.5 %collective-permute-start.5 = (bf16[1,13,256,128]{3,2,1,0:T(8,128)(2,1)}, bf16[1,13,256,128]{3,2,1,0:T(8,128)(2,1)S(1)}, u32[]{:S(2)}, u32[]{:S(2)}) collective-permute-start(bf16[1,13,256,128]{3,2,1,0:T(8,128)(2,1)} %get-tuple-element.14), channel_id=1, source_target_pairs={{0,6},{2,8},{4,10},{6,12},{8,14},{10,16},{12,18},{14,20},{16,22},{... | collective-permute-start | bytes 2555912 | tf_op jit(solution)/shard_map/ppermute | solution.py:10
  130.5 91.8 %collective-permute-start.4 = (bf16[1,12,256,128]{3,2,1,0:T(8,128)(2,1)}, bf16[1,12,256,128]{3,2,1,0:T(8,128)(2,1)}, u32[]{:S(2)}, u32[]{:S(2)}) collective-permute-start(bf16[1,12,256,128]{3,2,1,0:T(8,128)(2,1)} %get-tuple-element.12), channel_id=1, source_target_pairs={{0,8},{2,10},{4,12},{6,14},{8,16},{10,18},{12,20},{14,22},{16,24},... | collective-permute-start | bytes 2359304 | tf_op jit(solution)/shard_map/ppermute | solution.py:10
  149.8 72.5 %collective-permute-start.11 = (bf16[1,12,256,128]{3,2,1,0:T(8,128)(2,1)}, bf16[1,12,256,128]{3,2,1,0:T(8,128)(2,1)}, u32[]{:S(2)}, u32[]{:S(2)}) collective-permute-start(bf16[1,12,256,128]{3,2,1,0:T(8,128)(2,1)} %get-tuple-element.11), channel_id=1, source_target_pairs={{0,24},{2,26},{4,28},{6,30},{8,0},{10,2},{12,4},{14,6},{16,8},{18,... | collective-permute-start | bytes 2359304 | tf_op jit(solution)/shard_map/ppermute | solution.py:10
  150.2 60.7 %collective-permute-start.12 = (bf16[1,11,256,128]{3,2,1,0:T(8,128)(2,1)}, bf16[1,11,256,128]{3,2,1,0:T(8,128)(2,1)}, u32[]{:S(2)}, u32[]{:S(2)}) collective-permute-start(bf16[1,11,256,128]{3,2,1,0:T(8,128)(2,1)} %get-tuple-element.9), channel_id=1, source_target_pairs={{0,22},{2,24},{4,26},{6,28},{8,30},{10,0},{12,2},{14,4},{16,6},{18... | collective-permute-start | bytes 2162696 | tf_op jit(solution)/shard_map/ppermute | solution.py:10
  151.9 116.2 %collective-permute-start.10 = (bf16[1,13,256,128]{3,2,1,0:T(8,128)(2,1)}, bf16[1,13,256,128]{3,2,1,0:T(8,128)(2,1)}, u32[]{:S(2)}, u32[]{:S(2)}) collective-permute-start(bf16[1,13,256,128]{3,2,1,0:T(8,128)(2,1)} %get-tuple-element.13), channel_id=1, source_target_pairs={{0,26},{2,28},{4,30},{6,0},{8,2},{10,4},{12,6},{14,8},{16,10},{18,... | collective-permute-start | bytes 2555912 | tf_op jit(solution)/shard_map/ppermute | solution.py:10
  210.9 64.3 %collective-permute-start.6 = (bf16[1,14,256,128]{3,2,1,0:T(8,128)(2,1)}, bf16[1,14,256,128]{3,2,1,0:T(8,128)(2,1)}, u32[]{:S(2)}, u32[]{:S(2)}) collective-permute-start(bf16[1,14,256,128]{3,2,1,0:T(8,128)(2,1)} %get-tuple-element.16), channel_id=1, source_target_pairs={{0,4},{2,6},{4,8},{6,10},{8,12},{10,14},{12,16},{14,18},{16,20},{1... | collective-permute-start | bytes 2752520 | tf_op jit(solution)/shard_map/ppermute | solution.py:10
  222.3 64.5 %collective-permute-start.7 = (bf16[1,15,256,128]{3,2,1,0:T(8,128)(2,1)}, bf16[1,15,256,128]{3,2,1,0:T(8,128)(2,1)}, u32[]{:S(2)}, u32[]{:S(2)}) collective-permute-start(bf16[1,15,256,128]{3,2,1,0:T(8,128)(2,1)} %get-tuple-element.18), channel_id=1, source_target_pairs={{0,2},{2,4},{4,6},{6,8},{8,10},{10,12},{12,14},{14,16},{16,18},{18... | collective-permute-start | bytes 2949128 | tf_op jit(solution)/shard_map/ppermute | solution.py:10
  222.3 69.1 %collective-permute-start.8 = (bf16[1,15,256,128]{3,2,1,0:T(8,128)(2,1)}, bf16[1,15,256,128]{3,2,1,0:T(8,128)(2,1)}, u32[]{:S(2)}, u32[]{:S(2)}) collective-permute-start(bf16[1,15,256,128]{3,2,1,0:T(8,128)(2,1)} %get-tuple-element.17), channel_id=1, source_target_pairs={{0,30},{2,0},{4,2},{6,4},{8,6},{10,8},{12,10},{14,12},{16,14},{18,... | collective-permute-start | bytes 2949128 | tf_op jit(solution)/shard_map/ppermute | solution.py:10
  225.0 54.8 %collective-permute-start.9 = (bf16[1,14,256,128]{3,2,1,0:T(8,128)(2,1)}, bf16[1,14,256,128]{3,2,1,0:T(8,128)(2,1)}, u32[]{:S(2)}, u32[]{:S(2)}) collective-permute-start(bf16[1,14,256,128]{3,2,1,0:T(8,128)(2,1)} %get-tuple-element.15), channel_id=1, source_target_pairs={{0,28},{2,30},{4,0},{6,2},{8,4},{10,6},{12,8},{14,10},{16,12},{18,... | collective-permute-start | bytes 2752520 | tf_op jit(solution)/shard_map/ppermute | solution.py:10
  326.6 102.8 %collective-permute-start.16 = (bf16[1,9,256,128]{2,3,1,0:T(8,128)(2,1)S(1)}, bf16[1,9,256,128]{2,3,1,0:T(8,128)(2,1)S(1)}, u32[]{:S(2)}, u32[]{:S(2)}) collective-permute-start(bf16[1,9,256,128]{2,3,1,0:T(8,128)(2,1)S(1)} %get-tuple-element.20), channel_id=1, source_target_pairs={{0,14},{2,16},{4,18},{6,20},{8,22},{10,24},{12,26},{14,28},{16,30}... | collective-permute-start | bytes 1769480 | tf_op jit(solution)/shard_map/ppermute | solution.py:10
  327.9 101.6 %collective-permute-start.29 = (bf16[1,9,256,128]{2,3,1,0:T(8,128)(2,1)S(1)}, bf16[1,9,256,128]{2,3,1,0:T(8,128)(2,1)S(1)}, u32[]{:S(2)}, u32[]{:S(2)}) collective-permute-start(bf16[1,9,256,128]{2,3,1,0:T(8,128)(2,1)S(1)} %get-tuple-element.19), channel_id=1, source_target_pairs={{0,18},{2,20},{4,22},{6,24},{8,26},{10,28},{12,30},{14,0},{16,2},{... | collective-permute-start | bytes 1769480 | tf_op jit(solution)/shard_map/ppermute | solution.py:10
  329.5 99.1 %collective-permute-start.15 = (bf16[1,8,256,128]{2,3,1,0:T(8,128)(2,1)S(1)}, bf16[1,8,256,128]{2,3,1,0:T(8,128)(2,1)S(1)}, u32[]{:S(2)}, u32[]{:S(2)}) collective-permute-start(bf16[1,8,256,128]{2,3,1,0:T(8,128)(2,1)S(1)} %slice.120), channel_id=1, source_target_pairs={{0,16},{2,18},{4,20},{6,22},{8,24},{10,26},{12,28},{14,30},{16,0},... | collective-permute-start | bytes 1572872 | tf_op jit(solution)/shard_map/ppermute | solution.py:10
  331.3 120.2 %collective-permute-start.17 = (bf16[1,10,256,128]{2,3,1,0:T(8,128)(2,1)S(1)}, bf16[1,10,256,128]{2,3,1,0:T(8,128)(2,1)S(1)}, u32[]{:S(2)}, u32[]{:S(2)}) collective-permute-start(bf16[1,10,256,128]{2,3,1,0:T(8,128)(2,1)S(1)} %get-tuple-element.22), channel_id=1, source_target_pairs={{0,12},{2,14},{4,16},{6,18},{8,20},{10,22},{12,24},{14,26},{16,28}... | collective-permute-start | bytes 1966088 | tf_op jit(solution)/shard_map/ppermute | solution.py:10
  333.9 117.6 %collective-permute-start.28 = (bf16[1,10,256,128]{2,3,1,0:T(8,128)(2,1)S(1)}, bf16[1,10,256,128]{2,3,1,0:T(8,128)(2,1)S(1)}, u32[]{:S(2)}, u32[]{:S(2)}) collective-permute-start(bf16[1,10,256,128]{2,3,1,0:T(8,128)(2,1)S(1)} %get-tuple-element.21), channel_id=1, source_target_pairs={{0,20},{2,22},{4,24},{6,26},{8,28},{10,30},{12,0},{14,2},{16,4},{1... | collective-permute-start | bytes 1966088 | tf_op jit(solution)/shard_map/ppermute | solution.py:10
  429.4 51.9 %collective-permute-start.18 = (bf16[1,11,256,128]{2,3,1,0:T(8,128)(2,1)S(1)}, bf16[1,11,256,128]{2,3,1,0:T(8,128)(2,1)S(1)}, u32[]{:S(2)}, u32[]{:S(2)}) collective-permute-start(bf16[1,11,256,128]{2,3,1,0:T(8,128)(2,1)S(1)} %get-tuple-element.24), channel_id=1, source_target_pairs={{0,10},{2,12},{4,14},{6,16},{8,18},{10,20},{12,22},{14,24},{16,26}... | collective-permute-start | bytes 2162696 | tf_op jit(solution)/shard_map/ppermute | solution.py:10
  429.4 111.1 %collective-permute-start.19 = (bf16[1,12,256,128]{2,3,1,0:T(8,128)(2,1)S(1)}, bf16[1,12,256,128]{2,3,1,0:T(8,128)(2,1)}, u32[]{:S(2)}, u32[]{:S(2)}) collective-permute-start(bf16[1,12,256,128]{2,3,1,0:T(8,128)(2,1)S(1)} %get-tuple-element.26), channel_id=1, source_target_pairs={{0,8},{2,10},{4,12},{6,14},{8,16},{10,18},{12,20},{14,22},{16,24},... | collective-permute-start | bytes 2359304 | tf_op jit(solution)/shard_map/ppermute | solution.py:10
  430.5 110.1 %collective-permute-start.27 = (bf16[1,11,256,128]{2,3,1,0:T(8,128)(2,1)S(1)}, bf16[1,11,256,128]{2,3,1,0:T(8,128)(2,1)S(1)}, u32[]{:S(2)}, u32[]{:S(2)}) collective-permute-start(bf16[1,11,256,128]{2,3,1,0:T(8,128)(2,1)S(1)} %get-tuple-element.23), channel_id=1, source_target_pairs={{0,22},{2,24},{4,26},{6,28},{8,30},{10,0},{12,2},{14,4},{16,6},{18... | collective-permute-start | bytes 2162696 | tf_op jit(solution)/shard_map/ppermute | solution.py:10
  451.5 116.7 %copy-start.9 = (bf16[1,10,256,128]{2,3,1,0:T(8,128)(2,1)}, bf16[1,10,256,128]{2,3,1,0:T(8,128)(2,1)S(1)}, u32[]{:S(2)}) copy-start(bf16[1,10,256,128]{2,3,1,0:T(8,128)(2,1)S(1)} %collective-permute-done.17) | copy-start | bytes 1966084
  451.5 116.7 %collective-permute-start.20 = (bf16[1,13,256,128]{2,3,1,0:T(8,128)(2,1)S(1)}, bf16[1,13,256,128]{2,3,1,0:T(8,128)(2,1)S(1)}, u32[]{:S(2)}, u32[]{:S(2)}) collective-permute-start(bf16[1,13,256,128]{2,3,1,0:T(8,128)(2,1)S(1)} %get-tuple-element.28), channel_id=1, source_target_pairs={{0,6},{2,8},{4,10},{6,12},{8,14},{10,16},{12,18},{14,20},{16,22},{... | collective-permute-start | bytes 2555912 | tf_op jit(solution)/shard_map/ppermute | solution.py:10
  451.5 116.7 %copy-start.8 = (bf16[1,10,256,128]{2,3,1,0:T(8,128)(2,1)}, bf16[1,10,256,128]{2,3,1,0:T(8,128)(2,1)S(1)}, u32[]{:S(2)}) copy-start(bf16[1,10,256,128]{2,3,1,0:T(8,128)(2,1)S(1)} %collective-permute-done.28) | copy-start | bytes 1966084
  451.5 90.7 %collective-permute-start.26 = (bf16[1,12,256,128]{2,3,1,0:T(8,128)(2,1)S(1)}, bf16[1,12,256,128]{2,3,1,0:T(8,128)(2,1)S(1)}, u32[]{:S(2)}, u32[]{:S(2)}) collective-permute-start(bf16[1,12,256,128]{2,3,1,0:T(8,128)(2,1)S(1)} %get-tuple-element.25), channel_id=1, source_target_pairs={{0,24},{2,26},{4,28},{6,30},{8,0},{10,2},{12,4},{14,6},{16,8},{18,... | collective-permute-start | bytes 2359304 | tf_op jit(solution)/shard_map/ppermute | solution.py:10
  481.3 156.6 %collective-permute-start.21 = (bf16[1,14,256,128]{2,3,1,0:T(8,128)(2,1)}, bf16[1,14,256,128]{2,3,1,0:T(8,128)(2,1)}, u32[]{:S(2)}, u32[]{:S(2)}) collective-permute-start(bf16[1,14,256,128]{2,3,1,0:T(8,128)(2,1)} %get-tuple-element.30), channel_id=1, source_target_pairs={{0,4},{2,6},{4,8},{6,10},{8,12},{10,14},{12,16},{14,18},{16,20},{1... | collective-permute-start | bytes 2752520 | tf_op jit(solution)/shard_map/ppermute | solution.py:10
  540.5 102.3 %collective-permute-start.24 = (bf16[1,14,256,128]{2,3,1,0:T(8,128)(2,1)}, bf16[1,14,256,128]{2,3,1,0:T(8,128)(2,1)}, u32[]{:S(2)}, u32[]{:S(2)}) collective-permute-start(bf16[1,14,256,128]{2,3,1,0:T(8,128)(2,1)} %get-tuple-element.29), channel_id=1, source_target_pairs={{0,28},{2,30},{4,0},{6,2},{8,4},{10,6},{12,8},{14,10},{16,12},{18,... | collective-permute-start | bytes 2752520 | tf_op jit(solution)/shard_map/ppermute | solution.py:10
  540.6 89.4 %collective-permute-start.25 = (bf16[1,13,256,128]{2,3,1,0:T(8,128)(2,1)}, bf16[1,13,256,128]{2,3,1,0:T(8,128)(2,1)}, u32[]{:S(2)}, u32[]{:S(2)}) collective-permute-start(bf16[1,13,256,128]{2,3,1,0:T(8,128)(2,1)} %get-tuple-element.27), channel_id=1, source_target_pairs={{0,26},{2,28},{4,30},{6,0},{8,2},{10,4},{12,6},{14,8},{16,10},{18,... | collective-permute-start | bytes 2555912 | tf_op jit(solution)/shard_map/ppermute | solution.py:10
  542.2 108.2 %collective-permute-start.22 = (bf16[1,15,256,128]{2,3,1,0:T(8,128)(2,1)}, bf16[1,15,256,128]{2,3,1,0:T(8,128)(2,1)}, u32[]{:S(2)}, u32[]{:S(2)}) collective-permute-start(bf16[1,15,256,128]{2,3,1,0:T(8,128)(2,1)} %get-tuple-element.32), channel_id=1, source_target_pairs={{0,2},{2,4},{4,6},{6,8},{8,10},{10,12},{12,14},{14,16},{16,18},{18... | collective-permute-start | bytes 2949128 | tf_op jit(solution)/shard_map/ppermute | solution.py:10
  569.1 88.3 %collective-permute-start.23 = (bf16[1,15,256,128]{2,3,1,0:T(8,128)(2,1)}, bf16[1,15,256,128]{2,3,1,0:T(8,128)(2,1)}, u32[]{:S(2)}, u32[]{:S(2)}) collective-permute-start(bf16[1,15,256,128]{2,3,1,0:T(8,128)(2,1)} %get-tuple-element.31), channel_id=1, source_target_pairs={{0,30},{2,0},{4,2},{6,4},{8,6},{10,8},{12,10},{14,12},{16,14},{18,... | collective-permute-start | bytes 2949128 | tf_op jit(solution)/shard_map/ppermute | solution.py:10
  (13 other events, 307.9 us)
where the time goes:
time: 730 us; the launch traced here: 719 us
  waiting for transfers between devices  355 us (49%)
  local copies, waits for them, and re-layouts  227 us (31%)
  starting transfers between devices  91.8 us (13%)
  matrix products  19.3 us (3%)
  blocking collectives  18.1 us (2%)
    ppermute x30, waiting for transfers between devices, from_behind(): return lax.ppermute(value, axis, pairs)  355 us
    unnamed x74, local copies, waits for them, and re-layouts  97.1 us
    ppermute x30, starting transfers between devices, from_behind(): return lax.ppermute(value, axis, pairs)  91.8 us
    another operation x33, local copies, waits for them, and re-layouts, dense_terms(): jnp.stack([slot_shift(window[window_base + offset:window_base + offset +...  55.1 us
    concatenate x14, local copies, waits for them, and re-layouts, slot_shift(): jnp.concatenate([jnp.zeros_like(piece[:, :-delta]), piece[:, :band_width...  25 us
    concatenate x16, local copies, waits for them, and re-layouts, slot_shift(): jnp.concatenate([piece[:, delta:], jnp.zeros_like(piece[:, :delta])], axi...  24.2 us
    dot_general x2, matrix products, dense_terms(): jnp.einsum('ramcq,rascqn->crsmn', left_groups, right_groups, preferred_el...  19.3 us
    all_to_all x1, blocking collectives, per_device(): lax.all_to_all(column_slabs.astype(jnp.bfloat16), 'inner', split_axis=2,...  18.1 us
  transfers between devices with their start and end apart: 30, of which 8 were waited for; matrix products, arithmetic and copies ran while one was open for 23% of the time, Pallas kernels for 0%

commit v1 on v0

--- a/solution.py
+++ b/solution.py
@@ -1,7 +1,283 @@
+import functools
+
 import jax
 import jax.numpy as jnp
 from jax import lax
+from jax.experimental import pallas as pl
+from jax.experimental.pallas import tpu as pltpu
 from jax.sharding import PartitionSpec as P
+
+MESH = pl.DeviceIdType.MESH
+
+def grid_kernel(own, lane_live, out, other, panels, acc, pure, final,
+                left_send, left_recv, pass_send, pass_recv, panel_send, panel_recv, end_send, end_recv):
+    half, slots, block, _ = own.shape
+    slab = block // 2
+    width = slots * slab
+    rank, y = lax.axis_index("rows"), lax.axis_index("inner")
+    rows = lax.axis_size("rows")
+    core, x, z = rank % 2, (rank // 2) % 2, rank // 4
+    upper, low = z // 2, z % 2
+    parity = (upper + core) % 2
+    to_core, to_x, to_z = 1 - 2 * core, 1 - 2 * x, 1 - 2 * low
+    far_rank = lax.rem(rank + rows // 2, rows)
+    at_far = {"rows": far_rank, "inner": y}
+    at_y = {"rows": rank, "inner": 1 - y}
+    at_far_y = {"rows": far_rank, "inner": 1 - y}
+    at_z = {"rows": rank + 4 * to_z, "inner": y}
+    at_x = {"rows": rank + 2 * to_x, "inner": y}
+    at_core = {"rows": rank + to_core, "inner": y}
+    everyone = (at_far, at_y, at_far_y, at_z, at_x, at_core)
+
+    barrier = pltpu.get_barrier_semaphore()
+    for device in everyone:
+        pl.semaphore_signal(barrier, inc=1, device_id=device, device_id_type=MESH)
+
+    here = pl.ds(pl.multiple_of(y * slab, slab), slab)
+    there = pl.ds(pl.multiple_of((1 - y) * slab, slab), slab)
+    sent = []
+
+    def remote(source, target, send_sem, recv_sem, device):
+        return pltpu.make_async_remote_copy(
+            src_ref=source, dst_ref=target, send_sem=send_sem, recv_sem=recv_sem, device_id=device, device_id_type=MESH
+        )
+
+    def go(copy):
+        copy.start()
+        sent.append(copy)
+
+    pieces = 4
+    step = slots // pieces
+
+    def left_piece(ref, number, which, side):
+        if number == 0:
+            return ref.at[which, :, :, side]
+        return ref.at[which, (number - 1) * step : number * step, :, side]
+
+    def send_left(number):
+        which = 1 - parity if number == 0 else parity
+        go(remote(left_piece(own, number, which, here), left_piece(other, number, which, here),
+                  left_send.at[number], left_recv.at[number], at_far))
+
+    def pass_left(number):
+        which = parity if number == 0 else 1 - parity
+        mine = left_piece(other, number, which, here)
+        remote(mine, mine, left_send.at[number], left_recv.at[number], at_far).wait_recv()
+        go(remote(mine, mine, pass_send.at[number], pass_recv.at[number], at_y))
+
+    def end_left(number):
+        which = parity if number == 0 else 1 - parity
+        theirs = left_piece(other, number, which, there)
+        remote(theirs, theirs, pass_send.at[number], pass_recv.at[number], at_y).wait_recv()
+
+    def send_panel(product, source, target, send_at, device):
+        go(remote(panels.at[product, source], panels.at[product, target],
+                  panel_send.at[product, send_at], panel_recv.at[product, target], device))
+
+    def take(product, source):
+        ref = panels.at[product, source]
+        remote(ref, ref, panel_send.at[product, 0], panel_recv.at[product, source], at_core).wait_recv()
+
+    def share(product, source):
+        send_panel(product, source, 8 + source, 8 + source, at_core)
+
+    def spread(product, row):
+        send_panel(product, row, 2 + row, row, at_z)
+        send_panel(product, row, 4 + row, 2 + row, at_x)
+        share(product, row)
+
+    def mac(product, source, row, left):
+        chip_core, chip, far = source // 8, (source // 2) % 4, source % 2
+        delta = 4 * (to_z * (chip % 2) + 2 * far - 2 * row) + 2 * to_x * (chip // 2) + to_core * chip_core
+        slot = (delta + 8 + 2 * rows) % rows
+        shift = (slot + chip_core * (1 - 2 * parity)) // 2
+        block_left = left[slot % 2, slot // 2]
+        tile = 2 * slab
+        for part in range(width // tile):
+            lanes = pl.ds(pl.multiple_of(shift * slab + part * tile, slab), tile)
+            acc[row, :, lanes] += jnp.dot(
+                block_left, panels[product, source, :, part * tile : (part + 1) * tile],
+                preferred_element_type=jnp.float32,
+            )
+
+    middle = slice(slots // 2 * slab, slots // 2 * slab + width)
+
+    def masked_total(row):
+        return jnp.where(lane_live[row : row + 1, :] > 0, acc[row, :, middle], 0.0)
+
+    acc[...] = jnp.zeros_like(acc)
+    for u in range(slots):
+        panels[0, 0, :, u * slab : (u + 1) * slab] = own[parity, u, :, here]
+    pl.semaphore_wait(barrier, len(everyone))
+
+    send_left(0)
+    spread(0, 0)
+    for number in range(1, pieces + 1):
+        send_left(number)
+
+    def own_macs(sources):
+        first, gap, count = sources
+
+        def body(n, carry):
+            mac(0, first + gap * n, 0, own)
+            return carry
+
+        lax.fori_loop(0, count, body, 0)
+
+    own_macs((0, 1, 1))
+    take(0, 2)
+    send_panel(0, 2, 6, 4, at_x)
+    share(0, 2)
+    take(0, 4)
+    share(0, 4)
+    pass_left(0)
+    for u in range(slots):
+        panels[0, 1, :, u * slab : (u + 1) * slab] = other[parity, u, :, here]
+    spread(0, 1)
+
+
+    own_macs((1, 1, 2))
+    own_macs((4, 1, 1))
+    pass_left(1)
+    take(0, 6)
+    share(0, 6)
+    take(0, 8)
+    take(0, 10)
+    take(0, 12)
+    own_macs((6, 2, 4))
+    pass_left(2)
+    take(0, 3)
+    send_panel(0, 3, 7, 5, at_x)
+    share(0, 3)
+    pass_left(3)
+    take(0, 5)
+    share(0, 5)
+    take(0, 9)
+    take(0, 14)
+    own_macs((3, 2, 2))
+    own_macs((9, 5, 2))
+    pass_left(4)
+    take(0, 11)
+    take(0, 13)
+    own_macs((11, 2, 2))
+    take(0, 7)
+    share(0, 7)
+    own_macs((7, 8, 1))
+    take(0, 15)
+    own_macs((15, 1, 1))
+    panels[1, 0] = masked_total(0).astype(panels.dtype)
+    spread(1, 0)
+    acc[0] = jnp.zeros_like(acc[0])
+
+    for number in range(pieces + 1):
+        end_left(number)
+
+    def second_row(source, carry):
+        mac(0, source, 1, other)
+        return carry
+
+    lax.fori_loop(0, rows, second_row, 0)
+    panels[1, 1] = masked_total(1).astype(panels.dtype)
+    spread(1, 1)
+    acc[1] = jnp.zeros_like(acc[1])
+
+    def pair_macs(first, gap, count):
+        def body(n, carry):
+            mac(1, first + gap * n, 0, own)
+            mac(1, first + gap * n, 1, other)
+            return carry
+
+        lax.fori_loop(0, count, body, 0)
+
+    pair_macs(0, 1, 2)
+    take(1, 2)
+    send_panel(1, 2, 6, 4, at_x)
+    share(1, 2)
+    take(1, 4)
+    share(1, 4)
+    take(1, 8)
+    take(1, 9)
+    pair_macs(2, 2, 2)
+    pair_macs(8, 1, 2)
+    take(1, 5)
+    send_panel(1, 5, 7, 5, at_z)
+    share(1, 5)
+    take(1, 3)
+    share(1, 3)
+    take(1, 10)
+    take(1, 12)
+    pair_macs(3, 2, 2)
+    pair_macs(10, 2, 2)
+    take(1, 11)
+    take(1, 13)
+    pair_macs(11, 2, 2)
+    take(1, 6)
+    share(1, 6)
+    take(1, 7)
+    share(1, 7)
+    pair_macs(6, 1, 2)
+    take(1, 14)
+    take(1, 15)
+    pair_macs(14, 1, 2)
+
+    my_rows = pl.ds(pl.multiple_of(y * slab, slab), slab)
+    their_rows = pl.ds(pl.multiple_of((1 - y) * slab, slab), slab)
+    for row in (1, 0):
+        pure[row] = (3.0 * panels[1, row].astype(jnp.float32) - 2.0 * masked_total(row)).astype(pure.dtype)
+        if row == 1:
+            go(remote(pure.at[1, my_rows], final.at[1], end_send.at[1], end_recv.at[1], at_far))
+            go(remote(pure.at[1, their_rows], final.at[2], end_send.at[2], end_recv.at[2], at_far_y))
+    go(remote(pure.at[0, their_rows], final.at[0], end_send.at[0], end_recv.at[0], at_y))
+
+    def place(value, which, side):
+        for u in range(slots):
+            out[2 * u + which, :, side] = value[:, u * slab : (u + 1) * slab]
+
+    place(pure[0, my_rows], parity, here)
+    for number, which, side in ((0, parity, there), (1, 1 - parity, here), (2, 1 - parity, there)):
+        ref = final.at[number]
+        remote(ref, ref, end_send.at[number], end_recv.at[number], at_y).wait_recv()
+        place(final[number], which, side)
+    for copy in sent:
+        copy.wait_send()
+
+
+def on_grid(blocks, columns):
+    _, band_width, block_size, _ = blocks.shape
+    rows = lax.axis_size("rows")
+    slots, slab = band_width // 2, block_size // 2
+    width = slots * slab
+    rank = lax.axis_index("rows")
+    live = live_table(columns)
+    live_own = lax.dynamic_slice_in_dim(live, rank, 1, 0)[0]
+    live_far = lax.dynamic_slice_in_dim(live, lax.rem(rank + rows // 2, rows), 1, 0)[0]
+    parity = (rank // 8 + rank % 2) % 2
+    by_parity = jnp.stack([live_own, live_far]).reshape(2, slots, 2)
+    lane_live = jnp.where(parity == 0, by_parity[:, :, 0], by_parity[:, :, 1])
+    lane_live = jnp.repeat(lane_live.astype(jnp.float32), slab, axis=1)
+    masked = jnp.where(live_own[:, None, None], blocks[0], jnp.zeros_like(blocks[0]))
+    own = masked.reshape(slots, 2, block_size, block_size).transpose(1, 0, 2, 3)
+    vmem = pl.BlockSpec(memory_space=pltpu.VMEM)
+    dma = pltpu.SemaphoreType.DMA
+    result = pl.pallas_call(
+        grid_kernel,
+        out_shape=jax.ShapeDtypeStruct((band_width, slab, block_size), blocks.dtype),
+        in_specs=[vmem, vmem],
+        out_specs=vmem,
+        scratch_shapes=[
+            pltpu.VMEM((2, slots, block_size, block_size), blocks.dtype),
+            pltpu.VMEM((2, rows, block_size, width), blocks.dtype),
+            pltpu.VMEM((2, block_size, 2 * width), jnp.float32),
+            pltpu.VMEM((2, block_size, width), blocks.dtype),
+            pltpu.VMEM((3, slab, width), blocks.dtype),
+            dma((5,)), dma((5,)), dma((5,)), dma((5,)),
+            dma((2, 16)), dma((2, 16)), dma((3,)), dma((3,)),
+        ],
+        compiler_params=pltpu.CompilerParams(
+            collective_id=0, has_side_effects=True, vmem_limit_bytes=60 * 1024 * 1024
+        ),
+    )(own, lane_live)
+    return result[None].astype(jnp.float32)
 
 
 def from_behind(value, axis, steps):
@@ -115,6 +391,15 @@
 def solution(mesh):
     in_specs = (P("rows", None, None, None), P())
     out_specs = P("rows", None, "inner", None)
-    return jax.shard_map(
-        per_device, mesh=mesh, in_specs=in_specs, out_specs=out_specs, check_vma=False
-    )
+
+    def step(blocks, columns):
+        plain = mesh.shape["rows"] == 16 and mesh.shape["inner"] == 2
+        if plain and blocks.shape[:2] == (16, 16) and blocks.shape[2] % 256 == 0:
+            chosen = on_grid
+        else:
+            chosen = per_device
+        return jax.shard_map(chosen, mesh=mesh, in_specs=in_specs, out_specs=out_specs, check_vma=False)(
+            blocks, columns
+        )
+
+    return step

time: 730 us -> 142 us (0.19)
  the two profiles are of different devices: /device:TPU:10 before, /device:TPU:0 now
where the time goes in v1:
time: 142 us
  Pallas kernels  133 us (94%)
  other arithmetic  7.19 us (5%)
  local copies, waits for them, and re-layouts  2.15 us (2%)
    pallas_call x1, Pallas kernels, on_grid(): pl.pallas_call(grid_kernel, out_shape=jax.ShapeDtypeStruct((band_width, s...  133 us
    transpose x1, other arithmetic, on_grid(): own = masked.reshape(slots, 2, block_size, block_size).transpose(1, 0, 2, 3)  3.12 us

profile of v1, /device:TPU:0, one launch (start us, length us, event | category | flops | bytes accessed | tf_op | source)
XLA Modules:
  0.0 141.9 jit_solution(995160398104716616)
XLA Ops:
  0.0 1.1 compare_reduce_fusion
  1.1 0.5 broadcast.54
  1.7 0.7 fusion.2
  2.3 0.1 broadcast_in_dim.21
  2.4 0.1 copy.6
  2.5 0.1 reshape.42
  2.6 0.2 convert_reduce_fusion
  2.8 0.1 broadcast_bitcast_fusion
  2.9 0.6 copy.13
  3.5 3.1 %fusion.own = bf16[2,8,256,256]{3,2,1,0:T(8,128)(2,1)} fusion(bf16[8,2,256,256]{3,2,1,0:T(8,128)(2,1)} %bitcast.11, pred[8,2]{0,1:T(4,128)(4,1)S(1)} %copy.6), kind=kLoop, calls=%fused_computation.1 | loop fusion | flops 1048576 | bytes 4194320 | tf_op jit(solution)/shard_map/transpose | solution.py:259
  6.6 132.5 %shard_map.28 = bf16[16,128,256]{2,1,0:T(8,128)(2,1)} custom-call(bf16[2,8,256,256]{3,2,1,0:T(8,128)(2,1)} %fusion.own, f32[2,1024]{1,0:T(2,128)} %bitcast.12), custom_call_target="tpu_custom_call" | custom-call | tf_op jit(solution)/shard_map/pallas_call | solution.py:262
  139.1 2.8 %bitcast_convert_fusion = f32[1,16,128,256]{3,2,1,0:T(8,128)} fusion(bf16[16,128,256]{2,1,0:T(8,128)(2,1)} %shard_map.28), kind=kLoop, calls=%fused_computation.2 | loop fusion | flops 524288 | bytes 3145728 | tf_op jit(solution)/shard_map/convert_element_type | solution.py:280
  (2 shorter events, 0.0 us)

commit v2 on v0

--- a/solution.py
+++ b/solution.py
@@ -1,7 +1,329 @@
+import functools
+
 import jax
 import jax.numpy as jnp
 from jax import lax
+from jax.experimental import pallas as pl
+from jax.experimental.pallas import tpu as pltpu
 from jax.sharding import PartitionSpec as P
+
+MESH = pl.DeviceIdType.MESH
+
+def grid_kernel(columns, raw, out, own, other, lane_live, panels, acc, pure, final, load_sem,
+                left_send, left_recv, pass_send, pass_recv, panel_send, panel_recv, end_send, end_recv):
+    residues, depth, block, _ = own.shape
+    band = residues * depth
+    slab = block // 2
+    width = depth * slab
+    rank, y = lax.axis_index("rows"), lax.axis_index("inner")
+    rows = lax.axis_size("rows")
+    core, x, z = rank % 2, (rank // 2) % 2, rank // 4
+    upper, low = z // 2, z % 2
+    to_core, to_x, to_z = 1 - 2 * core, 1 - 2 * x, 1 - 2 * low
+    far_rank = lax.rem(rank + rows // 2, rows)
+    at_far = {"rows": far_rank, "inner": y}
+    at_y = {"rows": rank, "inner": 1 - y}
+    at_far_y = {"rows": far_rank, "inner": 1 - y}
+    at_z = {"rows": rank + 4 * to_z, "inner": y}
+    at_x = {"rows": rank + 2 * to_x, "inner": y}
+    at_core = {"rows": rank + to_core, "inner": y}
+    everyone = (at_far, at_y, at_far_y, at_z, at_x, at_core)
+
+    barrier = pltpu.get_barrier_semaphore()
+    for device in everyone:
+        pl.semaphore_signal(barrier, inc=1, device_id=device, device_id_type=MESH)
+
+    here = pl.ds(pl.multiple_of(y * slab, slab), slab)
+    there = pl.ds(pl.multiple_of((1 - y) * slab, slab), slab)
+    loads = [pltpu.make_async_copy(raw.at[:, which], own.at[which], load_sem.at[which]) for which in range(residues)]
+    for load in loads:
+        load.start()
+    sent = []
+    classes = (0, 1)
+
+    def residue(side, q, x_at, core_at):
+        return (side + 2 * q + 2 * residues - 2 * x_at - core_at) % residues
+
+    mine = [residue(upper, q, x, core) for q in classes]
+    fars = [residue(1 - upper, q, x, core) for q in classes]
+
+    def is_live(row_at, slot):
+        target = (row_at + slot + rows - band // 2) % rows
+        found = columns[row_at, 0] == target
+        for at in range(1, columns.shape[1]):
+            found = found | (columns[row_at, at] == target)
+        return jnp.where(found, 1, 0)
+
+    def remote(source, target, send_sem, recv_sem, device):
+        return pltpu.make_async_remote_copy(
+            src_ref=source, dst_ref=target, send_sem=send_sem, recv_sem=recv_sem, device_id=device, device_id_type=MESH
+        )
+
+    def go(copy):
+        copy.start()
+        sent.append(copy)
+
+    def send_left(number):
+        which = (fars + mine)[number]
+        go(remote(own.at[which, :, :, here], other.at[which, :, :, here],
+                  left_send.at[number], left_recv.at[number], at_far))
+
+    def pass_left(number):
+        ref = other.at[(mine + fars)[number], :, :, here]
+        remote(ref, ref, left_send.at[number], left_recv.at[number], at_far).wait_recv()
+        go(remote(ref, ref, pass_send.at[number], pass_recv.at[number], at_y))
+
+    def end_left(number):
+        ref = other.at[(mine + fars)[number], :, :, there]
+        remote(ref, ref, pass_send.at[number], pass_recv.at[number], at_y).wait_recv()
+
+    def send_panel(product, q, source, target, send_at, device):
+        go(remote(panels.at[product, q, source], panels.at[product, q, target],
+                  panel_send.at[product, q, send_at], panel_recv.at[product, q, target], device))
+
+    def share(product, q, source):
+        send_panel(product, q, source, 8 + source, 8 + source, at_core)
+
+    def take(product, q, source):
+        ref = panels.at[product, q, source]
+        remote(ref, ref, panel_send.at[product, q, 0], panel_recv.at[product, q, source], at_core).wait_recv()
+        if source < 8:
+            share(product, q, source)
+
+    def spread(product, q, row):
+        send_panel(product, q, row, 2 + row, row, at_z)
+        send_panel(product, q, row, 4 + row, 2 + row, at_x)
+        share(product, q, row)
+
+    def mac(product, q, source, row, left):
+        chip_core, chip, far = source // 8, (source // 2) % 4, source % 2
+        delta = 4 * (to_z * (chip % 2) + 2 * far - 2 * row) + 2 * to_x * (chip // 2) + to_core * chip_core
+        slot = (delta + band // 2 + 2 * rows) % rows
+        theirs = residue(upper, q, x + to_x * (chip // 2), core + to_core * chip_core)
+        shift = (theirs - mine[q] + slot) // residues
+        block_left = left[slot % residues, slot // residues]
+        tile = 2 * slab
+        for part in range(width // tile):
+            lanes = pl.ds(pl.multiple_of(shift * slab + part * tile, slab), tile)
+            acc[row, q, :, lanes] += jnp.dot(
+                block_left, panels[product, q, source, :, part * tile : (part + 1) * tile],
+                preferred_element_type=jnp.float32,
+            )
+
+    middle = slice(depth // 2 * slab, depth // 2 * slab + width)
+
+    def masked_total(row, q):
+        keep = lane_live[row : row + 1, q * width : (q + 1) * width] > 0
+        return jnp.where(keep, acc[row, q, :, middle], 0.0)
+
+    acc[...] = jnp.zeros_like(acc)
+    for row, row_at in enumerate((rank, far_rank)):
+        for q in classes:
+            for w in range(depth):
+                first = q * width + w * slab
+                live = is_live(row_at, residues * w + mine[q])
+                lane_live[row : row + 1, first : first + slab] = jnp.full((1, slab), live)
+
+    def mask_slot(slot, carry):
+        which, w = slot % residues, slot // residues
+        keep = jnp.full((1, block), is_live(rank, slot)) > 0
+        value = own[which, w]
+        own[which, w] = jnp.where(keep, value, jnp.zeros_like(value))
+        return carry
+
+    def fill(q, row, left):
+        for w in range(depth):
+            panels[0, q, row, :, w * slab : (w + 1) * slab] = left[mine[q], w, :, here]
+
+    for load in loads:
+        load.wait()
+    lax.fori_loop(0, band, mask_slot, 0)
+    for q in classes:
+        fill(q, 0, own)
+    pl.semaphore_wait(barrier, len(everyone))
+
+    for q in classes:
+        spread(0, q, 0)
+        send_left(q)
+
+    def own_macs(q, first, gap, count):
+        def body(n, carry):
+            mac(0, q, first + gap * n, 0, own)
+            return carry
+
+        lax.fori_loop(0, count, body, 0)
+
+    def both_own_macs(first, gap, count):
+        def body(n, carry):
+            for q in classes:
+                mac(0, q, first + gap * n, 0, own)
+            return carry
+
+        lax.fori_loop(0, count, body, 0)
+
+    both_own_macs(0, 1, 1)
+    for q in classes:
+        take(0, q, 2)
+        send_panel(0, q, 2, 6, 4, at_x)
+        take(0, q, 4)
+        pass_left(q)
+        fill(q, 1, other)
+        spread(0, q, 1)
+    send_left(2)
+    send_left(3)
+    for q in classes:
+        for source in (8, 9, 10, 12):
+            take(0, q, source)
+    both_own_macs(1, 1, 2)
+    both_own_macs(8, 1, 3)
+    take(0, 0, 6)
+    for q in classes:
+        take(0, q, 3)
+        send_panel(0, q, 3, 7, 5, at_x)
+        take(0, q, 5)
+    take(0, 1, 6)
+    both_own_macs(3, 1, 4)
+    for q in classes:
+        for source in (11, 13, 14):
+            take(0, q, source)
+    both_own_macs(11, 1, 4)
+    pass_left(2)
+    pass_left(3)
+
+    def second_row(q):
+        def body(source, carry):
+            mac(0, q, source, 1, other)
+            return carry
+
+        lax.fori_loop(0, rows, body, 0)
+
+    def square(row, q):
+        panels[1, q, row] = masked_total(row, q).astype(panels.dtype)
+        acc[row, q] = jnp.zeros_like(acc[row, q])
+
+    def last_own(q):
+        take(0, q, 7)
+        take(0, q, 15)
+        own_macs(q, 7, 8, 2)
+        square(0, q)
+
+    def pair_macs(q, first, gap, count):
+        def body(n, carry):
+            mac(1, q, first + gap * n, 0, own)
+            mac(1, q, first + gap * n, 1, other)
+            return carry
+
+        lax.fori_loop(0, count, body, 0)
+
+    last_own(0)
+    spread(1, 0, 0)
+    for number in range(residues):
+        end_left(number)
+    second_row(0)
+    square(1, 0)
+    spread(1, 0, 1)
+    last_own(1)
+    take(1, 0, 2)
+    send_panel(1, 0, 2, 6, 4, at_x)
+    spread(1, 1, 0)
+    second_row(1)
+    square(1, 1)
+    take(1, 0, 4)
+    take(1, 0, 8)
+    take(1, 0, 9)
+    take(1, 0, 5)
+    send_panel(1, 0, 5, 7, 5, at_z)
+    spread(1, 1, 1)
+
+    def finish(q):
+        for row in (1, 0):
+            total = 3.0 * panels[1, q, row].astype(jnp.float32) - 2.0 * masked_total(row, q)
+            pure[row, q] = total.astype(pure.dtype)
+            if row == 1:
+                go(remote(pure.at[1, q, here], final.at[1, q], end_send.at[1, q], end_recv.at[1, q], at_far))
+                go(remote(pure.at[1, q, there], final.at[2, q], end_send.at[2, q], end_recv.at[2, q], at_far_y))
+        go(remote(pure.at[0, q, there], final.at[0, q], end_send.at[0, q], end_recv.at[0, q], at_y))
+
+    pair_macs(0, 0, 1, 2)
+    pair_macs(0, 8, 1, 2)
+    pair_macs(0, 2, 2, 2)
+    take(1, 0, 3)
+    take(1, 0, 10)
+    take(1, 0, 12)
+    pair_macs(0, 3, 2, 2)
+    pair_macs(0, 10, 2, 2)
+    take(1, 1, 2)
+    send_panel(1, 1, 2, 6, 4, at_x)
+    take(1, 0, 6)
+    take(1, 0, 7)
+    pair_macs(0, 6, 1, 2)
+    for source in (11, 13, 14, 15):
+        take(1, 0, source)
+    pair_macs(0, 11, 2, 2)
+    pair_macs(0, 14, 1, 2)
+    finish(0)
+    take(1, 1, 4)
+    take(1, 1, 5)
+    send_panel(1, 1, 5, 7, 5, at_z)
+    take(1, 1, 3)
+    for source in (8, 9, 10, 12):
+        take(1, 1, source)
+    pair_macs(1, 0, 1, 6)
+    pair_macs(1, 8, 1, 3)
+    take(1, 1, 11)
+    take(1, 1, 13)
+    pair_macs(1, 11, 1, 3)
+    for source in (6, 7, 14, 15):
+        take(1, 1, source)
+    pair_macs(1, 6, 1, 2)
+    pair_macs(1, 14, 1, 2)
+    finish(1)
+
+    def place(value, which, side):
+        for w in range(depth):
+            out[residues * w + which, :, side] = value[:, w * slab : (w + 1) * slab]
+
+    for q in classes:
+        place(pure[0, q, here], mine[q], here)
+    for q in classes:
+        for number, which, side in ((0, mine[q], there), (1, fars[q], here), (2, fars[q], there)):
+            ref = final.at[number, q]
+            remote(ref, ref, end_send.at[number, q], end_recv.at[number, q], at_y).wait_recv()
+            place(final[number, q], which, side)
+    for copy in sent:
+        copy.wait_send()
+
+
+def on_grid(blocks, columns):
+    _, band_width, block_size, _ = blocks.shape
+    rows = lax.axis_size("rows")
+    residues = 4
+    depth, slab = band_width // residues, block_size // 2
+    width = depth * slab
+    raw = blocks.reshape(depth, residues, block_size, block_size)
+    vmem = pl.BlockSpec(memory_space=pltpu.VMEM)
+    dma = pltpu.SemaphoreType.DMA
+    result = pl.pallas_call(
+        grid_kernel,
+        out_shape=jax.ShapeDtypeStruct((band_width, slab, block_size), blocks.dtype),
+        in_specs=[pl.BlockSpec(memory_space=pltpu.SMEM), pl.BlockSpec(memory_space=pl.ANY)],
+        out_specs=vmem,
+        scratch_shapes=[
+            pltpu.VMEM((residues, depth, block_size, block_size), blocks.dtype),
+            pltpu.VMEM((residues, depth, block_size, block_size), blocks.dtype),
+            pltpu.VMEM((2, 2 * width), jnp.int32),
+            pltpu.VMEM((2, 2, rows, block_size, width), blocks.dtype),
+            pltpu.VMEM((2, 2, block_size, 2 * width), jnp.float32),
+            pltpu.VMEM((2, 2, block_size, width), blocks.dtype),
+            pltpu.VMEM((3, 2, slab, width), blocks.dtype),
+            dma((4,)), dma((4,)), dma((4,)), dma((4,)), dma((4,)),
+            dma((2, 2, 16)), dma((2, 2, 16)), dma((3, 2)), dma((3, 2)),
+        ],
+        compiler_params=pltpu.CompilerParams(
+            collective_id=0, has_side_effects=True, vmem_limit_bytes=60 * 1024 * 1024
+        ),
+    )(columns, raw)
+    return result[None].astype(jnp.float32)
 
 
 def from_behind(value, axis, steps):
@@ -115,6 +437,15 @@
 def solution(mesh):
     in_specs = (P("rows", None, None, None), P())
     out_specs = P("rows", None, "inner", None)
-    return jax.shard_map(
-        per_device, mesh=mesh, in_specs=in_specs, out_specs=out_specs, check_vma=False
-    )
+
+    def step(blocks, columns):
+        plain = mesh.shape["rows"] == 16 and mesh.shape["inner"] == 2
+        if plain and blocks.shape[:2] == (16, 16) and blocks.shape[2] % 256 == 0:
+            chosen = on_grid
+        else:
+            chosen = per_device
+        return jax.shard_map(chosen, mesh=mesh, in_specs=in_specs, out_specs=out_specs, check_vma=False)(
+            blocks, columns
+        )
+
+    return step

time: 730 us -> 128 us (0.18)
  the two profiles are of different devices: /device:TPU:10 before, /device:TPU:25 now
where the time goes in v2:
time: 128 us; the launch traced here: 127 us
  Pallas kernels  125 us (98%)
  other arithmetic  2.77 us (2%)
    pallas_call x1, Pallas kernels, on_grid(): pl.pallas_call(grid_kernel, out_shape=jax.ShapeDtypeStruct((band_width, s...  125 us
    convert_element_type x1, other arithmetic, on_grid(): return result[None].astype(jnp.float32)  2.77 us

profile of v2, /device:TPU:25, one launch (start us, length us, event | category | flops | bytes accessed | tf_op | source)
XLA Modules:
  0.0 127.5 jit_solution(13293709900523125919)
XLA Ops:
  0.0 124.7 %shard_map.28 = bf16[16,128,256]{2,1,0:T(8,128)(2,1)} custom-call(s32[16,16]{1,0:T(8,128)} %columns.1, bf16[4,4,256,256]{3,2,1,0:T(8,128)(2,1)} %bitcast.4), custom_call_target="tpu_custom_call" | custom-call | tf_op jit(solution)/shard_map/pallas_call | solution.py:306
  124.7 2.8 %bitcast_convert_fusion = f32[1,16,128,256]{3,2,1,0:T(8,128)} fusion(bf16[16,128,256]{2,1,0:T(8,128)(2,1)} %shard_map.28), kind=kLoop, calls=%fused_computation | loop fusion | flops 524288 | bytes 3145728 | tf_op jit(solution)/shard_map/convert_element_type | solution.py:326

commit v3 on v2

--- a/solution.py
+++ b/solution.py
@@ -143,8 +143,8 @@
     pl.semaphore_wait(barrier, len(everyone))
 
     for q in classes:
+        send_left(q)
         spread(0, q, 0)
-        send_left(q)
 
     def own_macs(q, first, gap, count):
         def body(n, carry):

time: 128 us -> 127 us (level)
  the two profiles are of different devices: /device:TPU:25 before, /device:TPU:0 now
where the time goes in v3:
time: 127 us
  Pallas kernels  124 us (98%)
  other arithmetic  2.77 us (2%)
    pallas_call x1, Pallas kernels, on_grid(): pl.pallas_call(grid_kernel, out_shape=jax.ShapeDtypeStruct((band_width, s...  124 us
    convert_element_type x1, other arithmetic, on_grid(): return result[None].astype(jnp.float32)  2.77 us

profile of v3, /device:TPU:0, one launch (start us, length us, event | category | flops | bytes accessed | tf_op | source)
XLA Modules:
  0.0 126.5 jit_solution(737204378842706414)
XLA Ops:
  0.0 123.7 %shard_map.28 = bf16[16,128,256]{2,1,0:T(8,128)(2,1)} custom-call(s32[16,16]{1,0:T(8,128)} %columns.1, bf16[4,4,256,256]{3,2,1,0:T(8,128)(2,1)} %bitcast.4), custom_call_target="tpu_custom_call" | custom-call | tf_op jit(solution)/shard_map/pallas_call | solution.py:306
  123.7 2.8 %bitcast_convert_fusion = f32[1,16,128,256]{3,2,1,0:T(8,128)} fusion(bf16[16,128,256]{2,1,0:T(8,128)(2,1)} %shard_map.28), kind=kLoop, calls=%fused_computation | loop fusion | flops 524288 | bytes 3145728 | tf_op jit(solution)/shard_map/convert_element_type | solution.py:326
